TPU v7x, 32 devices: a whole 2x2x4 slice. The times are simulated.
32 devices in a mesh: grp: 2 (over y), tx: 4 (over z), ty: 4 (over x, core).
Axes of the slice: x: 2, y: 2, z: 4, core: 2. Of those that a mesh axis runs over, the one named last changes fastest.
Arguments:
- obj_field: float32 [2, 1024, 512], P(None, ('grp', 'tx'), 'ty'), parts along dimension 1, may hold values from -6 to 6
- eigenprobes: bfloat16 [2, 32, 128, 128], P(None, 'grp'), parts along dimension 1, may hold values from -1.5 to 1.5
- weights: float32 [8, 4, 3, 16], P(('grp', 'tx'), 'ty'), parts along dimension 0, may hold values from -4 to 4
- offsets: int32 [8, 4, 3, 2], P(('grp', 'tx'), 'ty'), parts along dimension 0, may hold values from 0 to 127
- counts: int32 [8, 4], P(('grp', 'tx'), 'ty'), parts along dimension 0, may hold values from 1 to 3, as said below
- amplitudes: bfloat16 [8, 4, 3, 128, 128], P(('grp', 'tx'), 'ty'), parts along dimension 0, may hold values from 0.19921875 to 3
Outputs:
- new_object: float32 [2, 1024, 512], P(None, ('grp', 'tx'), 'ty'), parts along dimension 1
- new_eigenprobes: float32 [2, 32, 128, 128], P(None, 'grp'), parts along dimension 1
There are 2 independent parts, one for each index of `grp`. A program takes and returns all parts, laid end to end along the dimension named above; each array names one. Nothing has to cross between parts.
Inputs may be any that keep to these rules, and one draw needn't show every extreme that they name: Every tile holds 1 to 3 positions; some tile holds exactly 3; slots from counts on are unused.
All inputs are finite; a program needn't handle non-finite values.
Results may differ from a plain program's by a relative error of at most 0.0003.
Values sent between devices are 32-bit elements; how exact they have to be, the bound alone decides.
A program may use at most 64 MiB of HBM per device.

v0:
```python
import math
import jax
import jax.numpy as jnp
from jax import lax
from jax.sharding import PartitionSpec as P

high = lax.Precision.HIGHEST


def from_behind(value, axis, steps):
    count = lax.axis_size(axis)
    pairs = [(source, (source + steps) % count) for source in range(count)]
    return lax.ppermute(value, axis, pairs)


def tables(frame, sign):
    grid = jnp.arange(frame, dtype=jnp.int32)
    phase = grid[:, None] * grid[None, :] % frame
    angle = phase.astype(jnp.float32) * (2.0 * math.pi / frame)
    scale = 1.0 / math.sqrt(frame)
    return (jnp.cos(angle) * scale, sign * jnp.sin(angle) * scale)


def transform(real_part, imag_part, table_re, table_im):
    left_re = jnp.einsum("jk,skl->sjl", table_re, real_part, precision=high) - jnp.einsum(
        "jk,skl->sjl", table_im, imag_part, precision=high
    )
    left_im = jnp.einsum("jk,skl->sjl", table_re, imag_part, precision=high) + jnp.einsum(
        "jk,skl->sjl", table_im, real_part, precision=high
    )
    out_re = jnp.einsum("sjk,kl->sjl", left_re, table_re, precision=high) - jnp.einsum(
        "sjk,kl->sjl", left_im, table_im, precision=high
    )
    out_im = jnp.einsum("sjk,kl->sjl", left_re, table_im, precision=high) + jnp.einsum(
        "sjk,kl->sjl", left_im, table_re, precision=high
    )
    return (out_re, out_im)


def row_divisor(norms, start, count, frame, modes):
    mode_of_row = (start + jnp.arange(count, dtype=jnp.int32)) // frame % modes
    match = mode_of_row[:, None] == jnp.arange(modes, dtype=jnp.int32)[None, :]
    return jnp.sum(jnp.where(match, norms[None, :] + 1.0, 0.0), axis=1)


def per_device(obj_field, eigenprobes, weights, offsets, counts, amplitudes):
    tile = obj_field.shape[1]
    modes = eigenprobes.shape[1]
    frame = eigenprobes.shape[2]
    slots = weights.shape[2]
    wts = weights[0, 0]
    offs = offsets[0, 0]
    live = (jnp.arange(slots, dtype=jnp.int32) < counts[0, 0]).astype(jnp.float32)
    local_norms = jnp.sum(live[:, None] * wts * wts, axis=0)
    below = from_behind(obj_field, "tx", -1)
    tall = jnp.concatenate([obj_field, below], axis=1)
    beside = from_behind(tall, "ty", -1)
    region = jnp.concatenate([tall, beside], axis=2)
    zero_index = jnp.int32(0)

    def read_window(row_start, col_start):
        return lax.dynamic_slice(region, (zero_index, row_start, col_start), (2, frame, frame))

    windows = jax.vmap(read_window)(offs[:, 0], offs[:, 1])
    win_re = windows[:, 0]
    win_im = windows[:, 1]
    eig32 = eigenprobes.astype(jnp.float32)
    probe = jnp.einsum("sk,ckij->csij", wts, eig32, precision=high)
    psi_re = probe[0] * win_re - probe[1] * win_im
    psi_im = probe[0] * win_im + probe[1] * win_re
    fwd_re, fwd_im = tables(frame, -1.0)
    spec_re, spec_im = transform(psi_re, psi_im, fwd_re, fwd_im)
    amps = amplitudes[0, 0].astype(jnp.float32)
    factor = (amps / jnp.sqrt(spec_re * spec_re + spec_im * spec_im + 0.25) - 1.0) * live[
        :, None, None
    ]
    inv_re, inv_im = tables(frame, 1.0)
    chi_re, chi_im = transform(spec_re * factor, spec_im * factor, inv_re, inv_im)
    obj_re = probe[0] * chi_re + probe[1] * chi_im
    obj_im = probe[0] * chi_im - probe[1] * chi_re
    power = (probe[0] * probe[0] + probe[1] * probe[1]) * live[:, None, None]
    pieces = jnp.stack([obj_re, obj_im, power], axis=1)

    def add_slot(slot, acc):
        row_start = offs[slot, 0]
        col_start = offs[slot, 1]
        piece = lax.dynamic_index_in_dim(pieces, slot, 0, keepdims=False)
        current = lax.dynamic_slice(acc, (zero_index, row_start, col_start), (3, frame, frame))
        return lax.dynamic_update_slice(acc, current + piece, (zero_index, row_start, col_start))

    acc = jnp.zeros((3, tile + frame, tile + frame), jnp.float32)
    acc = lax.fori_loop(0, slots, add_slot, acc)
    grad_re = win_re * chi_re + win_im * chi_im
    grad_im = win_re * chi_im - win_im * chi_re
    slot_grad = jnp.stack([grad_re, grad_im])
    spilled = from_behind(acc[:, :, tile:], "ty", 1)
    merged = acc[:, :, :tile].at[:, :, :frame].add(spilled)
    dropped = from_behind(merged[:, tile:, :], "tx", 1)
    totals = merged[:, :tile, :].at[:, :frame, :].add(dropped)
    local_illum = jnp.sum(totals[2])
    norms, illum_sum = lax.psum((local_norms, local_illum), ("tx", "ty"))
    cells = lax.axis_size("tx") * lax.axis_size("ty") * tile * tile
    mean_illum = illum_sum / cells
    new_object = obj_field + totals[:2] / (totals[2] + mean_illum)[None]
    flat_rows = 2 * modes * frame
    flat_eig = eig32.reshape(flat_rows, frame)
    gprobe = jnp.einsum("sk,csij->ckij", wts, slot_grad, precision=high)
    flat_grad = gprobe.reshape(flat_rows, frame)
    share_rows = flat_rows // (lax.axis_size("tx") * lax.axis_size("ty"))
    start = lax.axis_index(("tx", "ty")) * share_rows
    share = lax.psum_scatter(flat_grad, ("tx", "ty"), scatter_dimension=0, tiled=True)
    own = lax.dynamic_slice_in_dim(flat_eig, start, share_rows, 0)
    updated = own + share / row_divisor(norms, start, share_rows, frame, modes)[:, None]
    new_eig = lax.all_gather(updated, ("tx", "ty"), axis=0, tiled=True).reshape(
        2, modes, frame, frame
    )
    return (new_object, new_eig)


def solution(mesh):
    return jax.shard_map(
        per_device,
        mesh=mesh,
        in_specs=(
            P(None, ("grp", "tx"), "ty"),
            P(None, "grp", None, None),
            P(("grp", "tx"), "ty", None, None),
            P(("grp", "tx"), "ty", None, None),
            P(("grp", "tx"), "ty"),
            P(("grp", "tx"), "ty", None, None, None),
        ),
        out_specs=(P(None, ("grp", "tx"), "ty"), P(None, "grp", None, None)),
        check_vma=False,
    )
```

profile of v0, /device:TPU:0, one launch (start us, length us, event | category | flops | bytes accessed | tf_op | source)
XLA Modules:
  0.0 176.3 jit_solution(10866427820670619271)
XLA Ops:
  7.2 5.1 %collective-permute-start = (f32[2,128,128]{2,1,0:T(8,128)}, f32[2,128,128]{2,1,0:T(8,128)S(1)}, u32[]{:S(2)}, u32[]{:S(2)}) collective-permute-start(f32[2,128,128]{2,1,0:T(8,128)} %param.16), channel_id=1, source_target_pairs={{0,12},{4,0},{8,4},{12,8},{1,13},{5,1},{9,5},{13,9},{2,14},{6,2},{... | collective-permute-start | bytes 393224 | tf_op jit(solution)/shard_map/ppermute | solution.py:13
  13.9 0.9 constant_dynamic-update-slice_fusion.1
  15.6 2.2 %convolution_bitcast_fusion.1 = f32[2,3,128,128]{3,1,2,0:T(4,128)S(1)} fusion(bf16[2,16,128,128]{3,2,1,0:T(8,128)(2,1)} %param.17, f32[1,1,3,16]{3,1,2,0:T(1,128)} %param.18), kind=kOutput, calls=%fused_computation.7 | convolution fusion | flops 18874368 | bytes 1441984 | tf_op jit(solution)/shard_map/sk,ckij->csij/dot_general | solution.py:68
  17.8 1.7 collective-permute-done.1
  19.5 15.2 %while.19 = (s32[]{:T(128)}, f32[2,256,256]{2,1,0:T(8,128)S(1)}, s32[3,3]{1,0:T(4,128)S(1)}, f32[3,2,128,128]{3,0,2,1:T(4,128)S(1)}, s32[]{:T(128)}, /*index=5*/s32[]{:T(128)}) while((s32[]{:T(128)}, f32[2,256,256]{2,1,0:T(8,128)S(1)}, s32[3,3]{1,0:T(4,128)S(1)}, f32[3,2,128,128]{3,0,2,1:T(4,128)S(1)}, s32[]{:T(128)}, /*index=5*/s32[]{:T(128)}) %tuple.75), condition=%wide.while_cond.2, body=%wide.while_body.2.sunk | while | flops 2 | bytes 524421 | solution.py:62
  20.1 1.3 constant_dynamic-slice_fusion.12
  21.4 3.1 %dynamic-update-slice.11 = f32[3,2,128,128]{3,0,2,1:T(4,128)S(1)} dynamic-update-slice(f32[3,2,128,128]{3,0,2,1:T(4,128)S(1)} %get-tuple-element.253, f32[1,2,128,128]{3,0,2,1:T(1,128)S(1)} %bitcast.173, s32[]{:T(128)S(6)} %copy.157, s32[]{:T(128)} %constant.159.clone.1..sunk.1, s32[]{:T(128)} %constant.159.clone.1..sunk.1, s32[]{:T(128)} %constant.159.clone.1..sunk.1) | dynamic-update-slice | bytes 262148 | tf_op jit(solution)/shard_map/vmap()/gather
  25.1 1.3 constant_dynamic-slice_fusion.12
  26.4 3.1 %dynamic-update-slice.11 = f32[3,2,128,128]{3,0,2,1:T(4,128)S(1)} dynamic-update-slice(f32[3,2,128,128]{3,0,2,1:T(4,128)S(1)} %get-tuple-element.253, f32[1,2,128,128]{3,0,2,1:T(1,128)S(1)} %bitcast.173, s32[]{:T(128)S(6)} %copy.157, s32[]{:T(128)} %constant.159.clone.1..sunk.1, s32[]{:T(128)} %constant.159.clone.1..sunk.1, s32[]{:T(128)} %constant.159.clone.1..sunk.1) | dynamic-update-slice | bytes 262148 | tf_op jit(solution)/shard_map/vmap()/gather
  30.1 1.3 constant_dynamic-slice_fusion.12
  31.4 3.1 %dynamic-update-slice.11 = f32[3,2,128,128]{3,0,2,1:T(4,128)S(1)} dynamic-update-slice(f32[3,2,128,128]{3,0,2,1:T(4,128)S(1)} %get-tuple-element.253, f32[1,2,128,128]{3,0,2,1:T(1,128)S(1)} %bitcast.173, s32[]{:T(128)S(6)} %copy.157, s32[]{:T(128)} %constant.159.clone.1..sunk.1, s32[]{:T(128)} %constant.159.clone.1..sunk.1, s32[]{:T(128)} %constant.159.clone.1..sunk.1) | dynamic-update-slice | bytes 262148 | tf_op jit(solution)/shard_map/vmap()/gather
  46.3 2.1 %convolution_bitcast_fusion = f32[2,16,128,128]{3,1,2,0:T(8,128)S(1)} fusion(f32[1,3,128,128]{3,1,2,0:T(4,128)S(1)} %get-tuple-element.177, f32[1,3,128,128]{3,1,2,0:T(4,128)S(1)} %get-tuple-element.176, f32[1,1,3,16]{3,1,2,0:T(1,128)S(1)} %copy-done.3), kind=kOutput, calls=%fused_computation.6 | convolution fusion | flops 18972672 | bytes 2490560 | tf_op jit(solution)/shard_map/sk,csij->ckij/dot_general | solution.py:107
  48.4 1.9 %copy.84 = f32[2,16,128,128]{3,2,1,0:T(8,128)} copy(f32[2,16,128,128]{3,1,2,0:T(8,128)S(1)} %convolution_bitcast_fusion) | data formatting | bytes 4194304 | tf_op jit(solution)/shard_map/sk,csij->ckij/transpose | solution.py:107
  51.1 22.6 %while.18 = (s32[]{:T(128)}, f32[3,256,256]{2,1,0:T(8,128)S(1)}, s32[3,2]{0,1:T(2,128)S(1)}, f32[3,3,128,128]{3,0,2,1:T(4,128)S(1)}, s32[]{:T(128)}, /*index=5*/s32[]{:T(128)}, s32[]{:T(128)}) while((s32[]{:T(128)}, f32[3,256,256]{2,1,0:T(8,128)S(1)}, s32[3,2]{0,1:T(2,128)S(1)}, f32[3,3,128,128]{3,0,2,1:T(4,128)S(1)}, s32[]{:T(128)}, ...), condition=%wide.region_1.2_spmd, body=%wide.region_0.0_spmd.sunk | while | flops 49160 | bytes 1376445 | solution.py:92
  55.8 2.8 %dynamic_update_slice.8 = f32[3,256,256]{2,1,0:T(8,128)S(1)} dynamic-update-slice(f32[3,256,256]{2,1,0:T(8,128)S(1)} %get-tuple-element.270, f32[3,128,128]{2,1,0:T(8,128)S(1)} %dynamic-slice_add_fusion.2, s32[]{:T(128)} %constant.159.clone.1..sunk, s32[]{:T(128)S(6)} %select_n.170, s32[]{:T(128)S(6)} %select_n.171) | dynamic-update-slice | bytes 393220 | tf_op jit(solution)/shard_map/while/body/eval_jaxpr/dynamic_update_slice | solution.py:89
  63.4 2.7 %dynamic_update_slice.8 = f32[3,256,256]{2,1,0:T(8,128)S(1)} dynamic-update-slice(f32[3,256,256]{2,1,0:T(8,128)S(1)} %get-tuple-element.270, f32[3,128,128]{2,1,0:T(8,128)S(1)} %dynamic-slice_add_fusion.2, s32[]{:T(128)} %constant.159.clone.1..sunk, s32[]{:T(128)S(6)} %select_n.170, s32[]{:T(128)S(6)} %select_n.171) | dynamic-update-slice | bytes 393220 | tf_op jit(solution)/shard_map/while/body/eval_jaxpr/dynamic_update_slice | solution.py:89
  70.9 2.8 %dynamic_update_slice.8 = f32[3,256,256]{2,1,0:T(8,128)S(1)} dynamic-update-slice(f32[3,256,256]{2,1,0:T(8,128)S(1)} %get-tuple-element.270, f32[3,128,128]{2,1,0:T(8,128)S(1)} %dynamic-slice_add_fusion.2, s32[]{:T(128)} %constant.159.clone.1..sunk, s32[]{:T(128)S(6)} %select_n.170, s32[]{:T(128)S(6)} %select_n.171) | dynamic-update-slice | bytes 393220 | tf_op jit(solution)/shard_map/while/body/eval_jaxpr/dynamic_update_slice | solution.py:89
  73.7 2.3 %collective-permute-start.2 = (f32[3,256,128]{2,1,0:T(8,128)S(1)}, f32[3,256,128]{2,1,0:T(8,128)S(1)}, u32[]{:S(2)}, u32[]{:S(2)}) collective-permute-start(f32[3,256,128]{2,1,0:T(8,128)S(1)} %slice.92), channel_id=1, source_target_pairs={{0,1},{1,2},{2,3},{3,0},{4,5},{5,6},{6,7},{7,4},{8,9},{9,10},{10,1... | collective-permute-start | bytes 1179656 | tf_op jit(solution)/shard_map/ppermute | solution.py:13
  76.0 5.6 %collective-permute-done.2 = f32[3,256,128]{2,1,0:T(8,128)S(1)} collective-permute-done((f32[3,256,128]{2,1,0:T(8,128)S(1)}, f32[3,256,128]{2,1,0:T(8,128)S(1)}, u32[]{:S(2)}, u32[]{:S(2)}) %collective-permute-start.2) | collective-permute-done | bytes 393248 | tf_op jit(solution)/shard_map/ppermute | solution.py:13
  82.2 11.8 %collective-permute-done.3 = f32[3,128,128]{2,1,0:T(8,128)S(1)} collective-permute-done((f32[3,128,128]{2,1,0:T(8,128)S(1)}, f32[3,128,128]{2,1,0:T(8,128)S(1)}, u32[]{:S(2)}, u32[]{:S(2)}) %collective-permute-start.3) | collective-permute-done | bytes 196640 | tf_op jit(solution)/shard_map/ppermute | solution.py:13
  94.6 30.4 %all-reduce = (f32[]{:T(128)}, f32[16]{0:T(128)S(1)}) all-reduce(f32[]{:T(128)} %slice_reduce_fusion, f32[16]{0:T(128)S(1)} %fusion.80), channel_id=1, replica_groups=mesh['grp'=2,'tx'=4,'ty'=4] {'tx','ty'}, use_global_device_ids=true, to_apply=%region_3.4 | all-reduce | flops 17 | bytes 136 | tf_op jit(solution)/shard_map/psum | solution.py:101
  125.0 1.7 convert_add_fusion
  128.1 38.2 %all-gather.2.cloned.1.call-done = f32[4096,128]{1,0:T(8,128)} async-done(((f32[256,128]{1,0:T(8,128)}), f32[4096,128]{1,0:T(8,128)}) %all-gather.2.cloned.1.call-update) | async-done | bytes 2097168 | tf_op jit(solution)/shard_map/all_gather | solution.py:114
  166.3 3.1 %copy.169 = f32[2,16,128,128]{3,2,1,0:T(8,128)} copy(f32[2,16,128,128]{3,2,1,0:T(8,128)} %bitcast.175) | data formatting | bytes 4194304
  (73 shorter events, 20.5 us)
Async XLA Ops:
  7.2 117.9 %reduce-scatter.2.cloned.1.call-start = ((), (), s32[]{:S(2)}) async-start(), calls=%async_computation.1 | async-start | bytes 2228224 | tf_op jit(solution)/shard_map/reduce_scatter | solution.py:111
  7.2 8.2 %collective-permute-start = (f32[2,128,128]{2,1,0:T(8,128)}, f32[2,128,128]{2,1,0:T(8,128)S(1)}, u32[]{:S(2)}, u32[]{:S(2)}) collective-permute-start(f32[2,128,128]{2,1,0:T(8,128)} %param.16), channel_id=1, source_target_pairs={{0,12},{4,0},{8,4},{12,8},{1,13},{5,1},{9,5},{13,9},{2,14},{6,2},{... | collective-permute-start | bytes 393224 | tf_op jit(solution)/shard_map/ppermute | solution.py:13
  15.4 4.0 %collective-permute-start.1 = (f32[2,256,128]{2,1,0:T(8,128)S(1)}, f32[2,256,128]{2,1,0:T(8,128)S(1)}, u32[]{:S(2)}, u32[]{:S(2)}) collective-permute-start(f32[2,256,128]{2,1,0:T(8,128)S(1)} %constant_dynamic-update-slice_fusion), channel_id=1, source_target_pairs={{0,3},{1,0},{2,1},{3,2},{4,7},{5,4},{6,5},{7,6},{8,11},{9,8},{10,9... | collective-permute-start | bytes 786440 | tf_op jit(solution)/shard_map/ppermute | solution.py:13
  35.5 4.5 %copy-start.1 = (bf16[1,1,3,128,128]{4,3,2,1,0:T(8,128)(2,1)S(1)}, bf16[1,1,3,128,128]{4,3,2,1,0:T(8,128)(2,1)}, u32[]{:S(2)}) copy-start(bf16[1,1,3,128,128]{4,3,2,1,0:T(8,128)(2,1)} %param.21) | copy-start | bytes 294916
  43.6 2.7 %copy-start.3 = (f32[1,1,3,16]{3,1,2,0:T(1,128)S(1)}, f32[1,1,3,16]{3,1,2,0:T(1,128)}, u32[]{:S(2)}) copy-start(f32[1,1,3,16]{3,1,2,0:T(1,128)} %param.18) | copy-start | bytes 580
  50.4 0.7 copy-start.2
  50.4 115.9 %all-gather.2.cloned.1.call-start = ((), (), s32[]{:S(2)}) async-start(), calls=%async_computation.2 | async-start | bytes 2228224 | tf_op jit(solution)/shard_map/all_gather | solution.py:114
  73.7 53.7 %copy-start = (f32[2,128,128]{2,1,0:T(8,128)S(1)}, f32[2,128,128]{2,1,0:T(8,128)}, u32[]{:S(2)}) copy-start(f32[2,128,128]{2,1,0:T(8,128)} %param.16) | copy-start | bytes 393220
  73.7 7.9 %collective-permute-start.2 = (f32[3,256,128]{2,1,0:T(8,128)S(1)}, f32[3,256,128]{2,1,0:T(8,128)S(1)}, u32[]{:S(2)}, u32[]{:S(2)}) collective-permute-start(f32[3,256,128]{2,1,0:T(8,128)S(1)} %slice.92), channel_id=1, source_target_pairs={{0,1},{1,2},{2,3},{3,0},{4,5},{5,6},{6,7},{7,4},{8,9},{9,10},{10,1... | collective-permute-start | bytes 1179656 | tf_op jit(solution)/shard_map/ppermute | solution.py:13
  81.7 12.2 %collective-permute-start.3 = (f32[3,128,128]{2,1,0:T(8,128)S(1)}, f32[3,128,128]{2,1,0:T(8,128)S(1)}, u32[]{:S(2)}, u32[]{:S(2)}) collective-permute-start(f32[3,128,128]{2,1,0:T(8,128)S(1)} %slice.115), channel_id=1, source_target_pairs={{0,4},{4,8},{8,12},{12,0},{1,5},{5,9},{9,13},{13,1},{2,6},{6,10},{... | collective-permute-start | bytes 589832 | tf_op jit(solution)/shard_map/ppermute | solution.py:13
Sparse Core Ops, SparseCore 0:
  50.5 65.2 reduce-scatter.1
  126.8 39.4 all-gather.1
where the time goes:
time: 177 us; the launch traced here: 176 us
  waiting for transfers between devices  57.9 us (33%)
  local copies, waits for them, and re-layouts  32.4 us (18%)
  blocking collectives  30.4 us (17%)
  between operations  15.7 us (9%)
  matrix products  14.7 us (8%)
  loops' own time  11.7 us (7%)
  starting transfers between devices  8.01 us (5%)
  other arithmetic  5.48 us (3%)
    all_gather x1, waiting for transfers between devices, per_device(): lax.all_gather(updated, ('tx', 'ty'), axis=0, tiled=True)  38.2 us
    psum x1, blocking collectives, per_device(): norms, illum_sum = lax.psum((local_norms, local_illum), ('tx', 'ty'))  30.4 us
    ppermute x4, waiting for transfers between devices, from_behind(): return lax.ppermute(value, axis, pairs)  19.7 us
    gather x12, local copies, waits for them, and re-layouts  14.9 us
    another operation x1, loops' own time, per_device(): acc = lax.fori_loop(0, slots, add_slot, acc)  11.4 us
    dynamic_update_slice x3, local copies, waits for them, and re-layouts, add_slot(): lax.dynamic_update_slice(acc, current + piece, (zero_index, row_start, co...  8.27 us
    ppermute x4, starting transfers between devices, from_behind(): return lax.ppermute(value, axis, pairs)  7.93 us
    unnamed x11, local copies, waits for them, and re-layouts  4.42 us
  transfers between devices with their start and end apart: 6, of which 5 were waited for; matrix products, arithmetic and copies ran while one was open for 10% of the time, Pallas kernels for 0%

commit v1 on v0

--- a/solution.py
+++ b/solution.py
@@ -98,7 +98,7 @@
     dropped = from_behind(merged[:, tile:, :], "tx", 1)
     totals = merged[:, :tile, :].at[:, :frame, :].add(dropped)
     local_illum = jnp.sum(totals[2])
-    norms, illum_sum = lax.psum((local_norms, local_illum), ("tx", "ty"))
+    norms, illum_sum = lax.psum(lax.psum((local_norms, local_illum), "ty"), "tx")
     cells = lax.axis_size("tx") * lax.axis_size("ty") * tile * tile
     mean_illum = illum_sum / cells
     new_object = obj_field + totals[:2] / (totals[2] + mean_illum)[None]

time: 177 us -> 169 us (0.955)
  blocking collectives: 30.4 us -> 16.9 us
  waiting for transfers between devices: 57.9 us -> 64.2 us
    psum x1 -> x2, blocking collectives: 30.4 us -> 16.9 us  [the longest x1 10.7 us: per_device(): lax.psum(lax.psum((local_norms, local_illum), 'ty'), 'tx')]
    reduce_scatter x1, waiting for transfers between devices: 0.01 us -> 3.31 us  [per_device(): lax.psum_scatter(flat_grad, ('tx', 'ty'), scatter_dimension=0, tiled=True)]
    all_gather x1, waiting for transfers between devices: 38.2 us -> 40.2 us  [per_device(): lax.all_gather(updated, ('tx', 'ty'), axis=0, tiled=True)]
  transfers between devices with their start and end apart: 6 -> 6, of which waited for: 5 -> 6; matrix products, arithmetic and copies ran while one was open for 10% -> 10% of each run, Pallas kernels for 0% -> 0%
where the time goes in v1:
time: 169 us; the launch traced here: 168 us
  waiting for transfers between devices  64.2 us (38%)
  local copies, waits for them, and re-layouts  32.3 us (19%)
  blocking collectives  16.9 us (10%)
  between operations  15.7 us (9%)
  matrix products  14.7 us (9%)
  loops' own time  11.1 us (7%)
  starting transfers between devices  8 us (5%)
  other arithmetic  5.48 us (3%)
    all_gather x1, waiting for transfers between devices, per_device(): lax.all_gather(updated, ('tx', 'ty'), axis=0, tiled=True)  40.2 us
    ppermute x4, waiting for transfers between devices, from_behind(): return lax.ppermute(value, axis, pairs)  20.7 us
    gather x12, local copies, waits for them, and re-layouts  14.9 us
    another operation x1, loops' own time, per_device(): acc = lax.fori_loop(0, slots, add_slot, acc)  10.8 us
    psum x1, blocking collectives, per_device(): lax.psum(lax.psum((local_norms, local_illum), 'ty'), 'tx')  10.7 us
    dynamic_update_slice x3, local copies, waits for them, and re-layouts, add_slot(): lax.dynamic_update_slice(acc, current + piece, (zero_index, row_start, co...  8.27 us
    ppermute x4, starting transfers between devices, from_behind(): return lax.ppermute(value, axis, pairs)  7.92 us
    psum x1, blocking collectives, per_device(): lax.psum((local_norms, local_illum), 'ty')  6.27 us
  transfers between devices with their start and end apart: 6, of which 6 were waited for; matrix products, arithmetic and copies ran while one was open for 10% of the time, Pallas kernels for 0%

profile of v1, /device:TPU:0, one launch (start us, length us, event | category | flops | bytes accessed | tf_op | source)
XLA Modules:
  0.0 168.5 jit_solution(2958057151013392547)
XLA Ops:
  7.2 5.1 %collective-permute-start = (f32[2,128,128]{2,1,0:T(8,128)}, f32[2,128,128]{2,1,0:T(8,128)S(1)}, u32[]{:S(2)}, u32[]{:S(2)}) collective-permute-start(f32[2,128,128]{2,1,0:T(8,128)} %param.16), channel_id=1, source_target_pairs={{0,12},{4,0},{8,4},{12,8},{1,13},{5,1},{9,5},{13,9},{2,14},{6,2},{... | collective-permute-start | bytes 393224 | tf_op jit(solution)/shard_map/ppermute | solution.py:13
  15.6 2.2 %convolution_bitcast_fusion.1 = f32[2,3,128,128]{3,1,2,0:T(4,128)S(1)} fusion(bf16[2,16,128,128]{3,2,1,0:T(8,128)(2,1)} %param.17, f32[1,1,3,16]{3,1,2,0:T(1,128)} %param.18), kind=kOutput, calls=%fused_computation.7 | convolution fusion | flops 18874368 | bytes 1441984 | tf_op jit(solution)/shard_map/sk,ckij->csij/dot_general | solution.py:68
  17.8 1.7 collective-permute-done.1
  19.5 15.2 %while.19 = (s32[]{:T(128)}, f32[2,256,256]{2,1,0:T(8,128)S(1)}, s32[3,3]{1,0:T(4,128)S(1)}, f32[3,2,128,128]{3,0,2,1:T(4,128)S(1)}, s32[]{:T(128)}, /*index=5*/s32[]{:T(128)}) while((s32[]{:T(128)}, f32[2,256,256]{2,1,0:T(8,128)S(1)}, s32[3,3]{1,0:T(4,128)S(1)}, f32[3,2,128,128]{3,0,2,1:T(4,128)S(1)}, s32[]{:T(128)}, /*index=5*/s32[]{:T(128)}) %tuple.75), condition=%wide.while_cond.2, body=%wide.while_body.2.sunk | while | flops 2 | bytes 524421 | solution.py:62
  20.1 1.3 constant_dynamic-slice_fusion.12
  21.4 3.1 %dynamic-update-slice.11 = f32[3,2,128,128]{3,0,2,1:T(4,128)S(1)} dynamic-update-slice(f32[3,2,128,128]{3,0,2,1:T(4,128)S(1)} %get-tuple-element.255, f32[1,2,128,128]{3,0,2,1:T(1,128)S(1)} %bitcast.173, s32[]{:T(128)S(6)} %copy.157, s32[]{:T(128)} %constant.159.clone.1..sunk.1, s32[]{:T(128)} %constant.159.clone.1..sunk.1, s32[]{:T(128)} %constant.159.clone.1..sunk.1) | dynamic-update-slice | bytes 262148 | tf_op jit(solution)/shard_map/vmap()/gather
  25.1 1.3 constant_dynamic-slice_fusion.12
  26.4 3.1 %dynamic-update-slice.11 = f32[3,2,128,128]{3,0,2,1:T(4,128)S(1)} dynamic-update-slice(f32[3,2,128,128]{3,0,2,1:T(4,128)S(1)} %get-tuple-element.255, f32[1,2,128,128]{3,0,2,1:T(1,128)S(1)} %bitcast.173, s32[]{:T(128)S(6)} %copy.157, s32[]{:T(128)} %constant.159.clone.1..sunk.1, s32[]{:T(128)} %constant.159.clone.1..sunk.1, s32[]{:T(128)} %constant.159.clone.1..sunk.1) | dynamic-update-slice | bytes 262148 | tf_op jit(solution)/shard_map/vmap()/gather
  31.4 3.1 %dynamic-update-slice.11 = f32[3,2,128,128]{3,0,2,1:T(4,128)S(1)} dynamic-update-slice(f32[3,2,128,128]{3,0,2,1:T(4,128)S(1)} %get-tuple-element.255, f32[1,2,128,128]{3,0,2,1:T(1,128)S(1)} %bitcast.173, s32[]{:T(128)S(6)} %copy.157, s32[]{:T(128)} %constant.159.clone.1..sunk.1, s32[]{:T(128)} %constant.159.clone.1..sunk.1, s32[]{:T(128)} %constant.159.clone.1..sunk.1) | dynamic-update-slice | bytes 262148 | tf_op jit(solution)/shard_map/vmap()/gather
  46.3 2.1 %convolution_bitcast_fusion = f32[2,16,128,128]{3,1,2,0:T(8,128)S(1)} fusion(f32[1,3,128,128]{3,1,2,0:T(4,128)S(1)} %get-tuple-element.179, f32[1,3,128,128]{3,1,2,0:T(4,128)S(1)} %get-tuple-element.178, f32[1,1,3,16]{3,1,2,0:T(1,128)S(1)} %copy-done.3), kind=kOutput, calls=%fused_computation.6 | convolution fusion | flops 18972672 | bytes 2490560 | tf_op jit(solution)/shard_map/sk,csij->ckij/dot_general | solution.py:107
  48.4 1.9 %copy.84 = f32[2,16,128,128]{3,2,1,0:T(8,128)} copy(f32[2,16,128,128]{3,1,2,0:T(8,128)S(1)} %convolution_bitcast_fusion) | data formatting | bytes 4194304 | tf_op jit(solution)/shard_map/sk,csij->ckij/transpose | solution.py:107
  51.1 21.9 %while.18 = (s32[]{:T(128)}, f32[3,256,256]{2,1,0:T(8,128)S(1)}, s32[3,2]{0,1:T(2,128)S(1)}, f32[3,3,128,128]{3,0,2,1:T(4,128)S(1)}, s32[]{:T(128)}, /*index=5*/s32[]{:T(128)}, s32[]{:T(128)}) while((s32[]{:T(128)}, f32[3,256,256]{2,1,0:T(8,128)S(1)}, s32[3,2]{0,1:T(2,128)S(1)}, f32[3,3,128,128]{3,0,2,1:T(4,128)S(1)}, s32[]{:T(128)}, ...), condition=%wide.region_1.2_spmd, body=%wide.region_0.0_spmd.sunk | while | flops 49160 | bytes 1376445 | solution.py:92
  55.6 2.8 %dynamic_update_slice.8 = f32[3,256,256]{2,1,0:T(8,128)S(1)} dynamic-update-slice(f32[3,256,256]{2,1,0:T(8,128)S(1)} %get-tuple-element.272, f32[3,128,128]{2,1,0:T(8,128)S(1)} %dynamic-slice_add_fusion.2, s32[]{:T(128)} %constant.159.clone.1..sunk, s32[]{:T(128)S(6)} %select_n.170, s32[]{:T(128)S(6)} %select_n.171) | dynamic-update-slice | bytes 393220 | tf_op jit(solution)/shard_map/while/body/eval_jaxpr/dynamic_update_slice | solution.py:89
  62.9 2.7 %dynamic_update_slice.8 = f32[3,256,256]{2,1,0:T(8,128)S(1)} dynamic-update-slice(f32[3,256,256]{2,1,0:T(8,128)S(1)} %get-tuple-element.272, f32[3,128,128]{2,1,0:T(8,128)S(1)} %dynamic-slice_add_fusion.2, s32[]{:T(128)} %constant.159.clone.1..sunk, s32[]{:T(128)S(6)} %select_n.170, s32[]{:T(128)S(6)} %select_n.171) | dynamic-update-slice | bytes 393220 | tf_op jit(solution)/shard_map/while/body/eval_jaxpr/dynamic_update_slice | solution.py:89
  70.2 2.8 %dynamic_update_slice.8 = f32[3,256,256]{2,1,0:T(8,128)S(1)} dynamic-update-slice(f32[3,256,256]{2,1,0:T(8,128)S(1)} %get-tuple-element.272, f32[3,128,128]{2,1,0:T(8,128)S(1)} %dynamic-slice_add_fusion.2, s32[]{:T(128)} %constant.159.clone.1..sunk, s32[]{:T(128)S(6)} %select_n.170, s32[]{:T(128)S(6)} %select_n.171) | dynamic-update-slice | bytes 393220 | tf_op jit(solution)/shard_map/while/body/eval_jaxpr/dynamic_update_slice | solution.py:89
  73.1 2.3 %collective-permute-start.2 = (f32[3,256,128]{2,1,0:T(8,128)S(1)}, f32[3,256,128]{2,1,0:T(8,128)S(1)}, u32[]{:S(2)}, u32[]{:S(2)}) collective-permute-start(f32[3,256,128]{2,1,0:T(8,128)S(1)} %slice.92), channel_id=1, source_target_pairs={{0,1},{1,2},{2,3},{3,0},{4,5},{5,6},{6,7},{7,4},{8,9},{9,10},{10,1... | collective-permute-start | bytes 1179656 | tf_op jit(solution)/shard_map/ppermute | solution.py:13
  75.4 5.6 %collective-permute-done.2 = f32[3,256,128]{2,1,0:T(8,128)S(1)} collective-permute-done((f32[3,256,128]{2,1,0:T(8,128)S(1)}, f32[3,256,128]{2,1,0:T(8,128)S(1)}, u32[]{:S(2)}, u32[]{:S(2)}) %collective-permute-start.2) | collective-permute-done | bytes 393248 | tf_op jit(solution)/shard_map/ppermute | solution.py:13
  81.5 12.8 %collective-permute-done.3 = f32[3,128,128]{2,1,0:T(8,128)S(1)} collective-permute-done((f32[3,128,128]{2,1,0:T(8,128)S(1)}, f32[3,128,128]{2,1,0:T(8,128)S(1)}, u32[]{:S(2)}, u32[]{:S(2)}) %collective-permute-start.3) | collective-permute-done | bytes 196640 | tf_op jit(solution)/shard_map/ppermute | solution.py:13
  94.9 6.3 %all-reduce = (f32[]{:T(128)}, f32[16]{0:T(128)S(1)}) all-reduce(f32[]{:T(128)} %slice_reduce_fusion, f32[16]{0:T(128)S(1)} %fusion.80), channel_id=1, replica_groups=mesh['grp'=2,'tx'=4,'ty'=4] {'ty'}, use_global_device_ids=true, to_apply=%region_3.4 | all-reduce | flops 17 | bytes 136 | tf_op jit(solution)/shard_map/psum | solution.py:101
  101.2 10.7 %all-reduce.1 = (f32[]{:T(128)}, f32[16]{0:T(128)S(1)}) all-reduce(f32[]{:T(128)} %get-tuple-element.170, f32[16]{0:T(128)S(1)} %get-tuple-element.171), channel_id=1, replica_groups=mesh['grp'=2,'tx'=4,'ty'=4] {'tx'}, use_global_device_ids=true, to_apply=%region_4.5 | all-reduce | flops 17 | bytes 136 | tf_op jit(solution)/shard_map/psum | solution.py:101
  112.0 3.3 %reduce-scatter.2.cloned.1.call-done = f32[256,128]{1,0:T(8,128)} async-done(((f32[4096,128]{1,0:T(8,128)}), f32[256,128]{1,0:T(8,128)}) %reduce-scatter.2.cloned.1.call-update) | async-done | bytes 131088 | tf_op jit(solution)/shard_map/reduce_scatter | solution.py:111
  115.3 1.7 convert_add_fusion
  118.3 40.2 %all-gather.2.cloned.1.call-done = f32[4096,128]{1,0:T(8,128)} async-done(((f32[256,128]{1,0:T(8,128)}), f32[4096,128]{1,0:T(8,128)}) %all-gather.2.cloned.1.call-update) | async-done | bytes 2097168 | tf_op jit(solution)/shard_map/all_gather | solution.py:114
  158.5 3.1 %copy.169 = f32[2,16,128,128]{3,2,1,0:T(8,128)} copy(f32[2,16,128,128]{3,2,1,0:T(8,128)} %bitcast.175) | data formatting | bytes 4194304
  (74 shorter events, 22.6 us)
Async XLA Ops:
  7.2 108.1 %reduce-scatter.2.cloned.1.call-start = ((), (), s32[]{:S(2)}) async-start(), calls=%async_computation.1 | async-start | bytes 2228224 | tf_op jit(solution)/shard_map/reduce_scatter | solution.py:111
  7.2 8.2 %collective-permute-start = (f32[2,128,128]{2,1,0:T(8,128)}, f32[2,128,128]{2,1,0:T(8,128)S(1)}, u32[]{:S(2)}, u32[]{:S(2)}) collective-permute-start(f32[2,128,128]{2,1,0:T(8,128)} %param.16), channel_id=1, source_target_pairs={{0,12},{4,0},{8,4},{12,8},{1,13},{5,1},{9,5},{13,9},{2,14},{6,2},{... | collective-permute-start | bytes 393224 | tf_op jit(solution)/shard_map/ppermute | solution.py:13
  15.4 4.0 %collective-permute-start.1 = (f32[2,256,128]{2,1,0:T(8,128)S(1)}, f32[2,256,128]{2,1,0:T(8,128)S(1)}, u32[]{:S(2)}, u32[]{:S(2)}) collective-permute-start(f32[2,256,128]{2,1,0:T(8,128)S(1)} %constant_dynamic-update-slice_fusion), channel_id=1, source_target_pairs={{0,3},{1,0},{2,1},{3,2},{4,7},{5,4},{6,5},{7,6},{8,11},{9,8},{10,9... | collective-permute-start | bytes 786440 | tf_op jit(solution)/shard_map/ppermute | solution.py:13
  35.5 4.5 %copy-start.1 = (bf16[1,1,3,128,128]{4,3,2,1,0:T(8,128)(2,1)S(1)}, bf16[1,1,3,128,128]{4,3,2,1,0:T(8,128)(2,1)}, u32[]{:S(2)}) copy-start(bf16[1,1,3,128,128]{4,3,2,1,0:T(8,128)(2,1)} %param.21) | copy-start | bytes 294916
  43.6 2.7 %copy-start.3 = (f32[1,1,3,16]{3,1,2,0:T(1,128)S(1)}, f32[1,1,3,16]{3,1,2,0:T(1,128)}, u32[]{:S(2)}) copy-start(f32[1,1,3,16]{3,1,2,0:T(1,128)} %param.18) | copy-start | bytes 580
  50.4 0.7 copy-start.2
  50.4 108.1 %all-gather.2.cloned.1.call-start = ((), (), s32[]{:S(2)}) async-start(), calls=%async_computation.2 | async-start | bytes 2228224 | tf_op jit(solution)/shard_map/all_gather | solution.py:114
  73.0 44.6 %copy-start = (f32[2,128,128]{2,1,0:T(8,128)S(1)}, f32[2,128,128]{2,1,0:T(8,128)}, u32[]{:S(2)}) copy-start(f32[2,128,128]{2,1,0:T(8,128)} %param.16) | copy-start | bytes 393220
  73.1 7.9 %collective-permute-start.2 = (f32[3,256,128]{2,1,0:T(8,128)S(1)}, f32[3,256,128]{2,1,0:T(8,128)S(1)}, u32[]{:S(2)}, u32[]{:S(2)}) collective-permute-start(f32[3,256,128]{2,1,0:T(8,128)S(1)} %slice.92), channel_id=1, source_target_pairs={{0,1},{1,2},{2,3},{3,0},{4,5},{5,6},{6,7},{7,4},{8,9},{9,10},{10,1... | collective-permute-start | bytes 1179656 | tf_op jit(solution)/shard_map/ppermute | solution.py:13
  81.1 13.2 %collective-permute-start.3 = (f32[3,128,128]{2,1,0:T(8,128)S(1)}, f32[3,128,128]{2,1,0:T(8,128)S(1)}, u32[]{:S(2)}, u32[]{:S(2)}) collective-permute-start(f32[3,128,128]{2,1,0:T(8,128)S(1)} %slice.115), channel_id=1, source_target_pairs={{0,4},{4,8},{8,12},{12,0},{1,5},{5,9},{9,13},{13,1},{2,6},{6,10},{... | collective-permute-start | bytes 589832 | tf_op jit(solution)/shard_map/ppermute | solution.py:13
Sparse Core Ops, SparseCore 0:
  50.5 64.7 reduce-scatter.1
  118.0 40.4 all-gather.1
